TPU v7x, 32 devices: a whole 2x2x4 slice. The times are simulated.
32 devices in a mesh: dp: 4 (over x, core), section: 2 (over y), expert: 4 (over z).
Axes of the slice: x: 2, y: 2, z: 4, core: 2. Of those that a mesh axis runs over, the one named last changes fastest.
Arguments:
- paths_in: bfloat16 [2, 256, 4, 7168], P(None, 'expert', None, 'dp'), may hold values from -12 to 12
- path_proj: bfloat16 [2, 24, 4, 7168], P('section', None, None, 'dp'), may hold values from -0.03125 to 0.03125
- coef_bias: float32 [2, 24], P('section'), may hold values from -4 to 4
- norm_gain: bfloat16 [2, 7168], P('section', 'dp'), may hold values from 0.25 to 1.75
- w_gate_up: bfloat16 [2, 4, 7168, 2, 512], P('section', 'expert', 'dp'), may hold values from -0.0625 to 0.0625
- w_down: bfloat16 [2, 4, 512, 7168], P('section', 'expert', None, 'dp'), may hold values from -0.1875 to 0.1875
- routes: int32 [2, 2, 256, 1], P('section', None, 'expert'), may hold values from 0 to 1; in each aligned block of 64 rows (0 to 63, 64 to 127, ..., all dimensions but the last counted through in order) at most 32 rows name the same one
- route_gate: float32 [2, 2, 256, 1], P('section', None, 'expert'), may hold values from 0.2 to 1
Outputs:
- paths_out: bfloat16 [2, 2, 256, 4, 7168], P('section', None, 'expert', None, 'dp')
Inputs may be any that keep to these rules, and one draw needn't show every extreme that they name: `routes`: each row names exactly one expert. In each aligned block of 64 rows (the tokens of one index of expert in one layer and micro-batch) no expert is named more than 32 times, a bound that some block reaches.
All inputs are finite; a program needn't handle non-finite values.
Results may differ from a plain program's by a relative error of at most 0.014.
Values may be sent and summed in bfloat16 or wider, within the bound.
A program may use at most 64 MiB of HBM per device.

v0:
```python
import jax
import jax.numpy as jnp
from jax import lax
from jax.sharding import PartitionSpec as P

D = 7168
RESIDUAL_STREAMS = 4
SINK = 20


EPSILON = 1e-06


def passed_along(value, axis, steps):
    count = lax.axis_size(axis)
    leading, last = (max(0, -steps), min(count, count - steps))
    return lax.ppermute(value, axis, [(source, source + steps) for source in range(leading, last)])


def doubly_stochastic_project(stream_mixer):
    for repeat in range(SINK):
        stream_mixer = stream_mixer / jnp.sum(stream_mixer, axis=2, keepdims=True)
        stream_mixer = stream_mixer / jnp.sum(stream_mixer, axis=1, keepdims=True)
    return stream_mixer


def expert_block(received, gate_up, down_proj):
    sources, items, width = received.shape
    slot_rows = received.reshape(sources * items, width)
    inner = down_proj.shape[0]
    hidden_pre = jnp.dot(slot_rows, gate_up, preferred_element_type=jnp.float32)
    summed = lax.psum(hidden_pre, "dp")
    hidden = (jax.nn.silu(summed[:, :inner]) * summed[:, inner:]).astype(jnp.bfloat16)
    expert_output_rows = jnp.dot(hidden, down_proj, preferred_element_type=jnp.float32)
    expert_output_rows = expert_output_rows.astype(jnp.bfloat16).reshape(sources, items, width)
    return lax.all_to_all(expert_output_rows, "expert", split_axis=0, concat_axis=0, tiled=True)


def mix_layer(residual, path_proj, coef_bias, norm_gain, gate_up, down_proj, routes_now, gates_now):
    rows, paths, width = residual.shape
    widened = residual.astype(jnp.float32)
    square_part = jnp.sum(widened * widened, axis=(1, 2))
    projected = jnp.einsum("tsd,csd->tc", residual, path_proj, preferred_element_type=jnp.float32)
    path_gram = jnp.einsum("tid,tjd->tij", residual, residual, preferred_element_type=jnp.float32)
    square_sum, projected, path_gram = lax.psum((square_part, projected, path_gram), "dp")
    router_scores = (
        projected * lax.rsqrt(square_sum / (RESIDUAL_STREAMS * D) + EPSILON)[:, None]
        + coef_bias[None, :]
    )
    pre_weight = jax.nn.sigmoid(router_scores[:, :RESIDUAL_STREAMS])
    post_weight = 2.0 * jax.nn.sigmoid(router_scores[:, RESIDUAL_STREAMS : 2 * RESIDUAL_STREAMS])
    stream_mixer = doubly_stochastic_project(
        jnp.exp(router_scores[:, 2 * RESIDUAL_STREAMS :]).reshape(
            -1, RESIDUAL_STREAMS, RESIDUAL_STREAMS
        )
    )
    merged = jnp.sum(pre_weight[:, :, None] * widened, axis=1)
    width_sum = jnp.einsum(
        "ti,tij,tj->t", pre_weight, path_gram, pre_weight, precision=lax.Precision.HIGHEST
    )
    normed = (
        merged
        * lax.rsqrt(width_sum / D + EPSILON)[:, None]
        * norm_gain.astype(jnp.float32)[None, :]
    ).astype(jnp.bfloat16)
    expert_count = lax.axis_size("expert") // 2
    selected_expert_count = routes_now.shape[1]
    capacity = min(rows, max(2, (rows * selected_expert_count + expert_count - 1) // expert_count))
    slot_count = expert_count * capacity
    flat_routes = routes_now.reshape(-1)
    chosen = (flat_routes[:, None] == jnp.arange(expert_count, dtype=jnp.int32)[None, :]).astype(
        jnp.int32
    )
    earlier = jnp.cumsum(chosen, axis=0) - chosen
    rank_within = jnp.sum(earlier * chosen, axis=1)
    slot_of = flat_routes * capacity + rank_within
    slot_match = jnp.arange(slot_count, dtype=jnp.int32)[:, None] == slot_of[None, :]
    dispatch_map = jnp.sum(
        slot_match.reshape(slot_count, rows, selected_expert_count).astype(jnp.int32), axis=2
    ).astype(jnp.bfloat16)
    gate_spread = jnp.where(slot_match, gates_now.reshape(-1)[None, :], 0.0)
    combine_map = jnp.sum(gate_spread.reshape(slot_count, rows, selected_expert_count), axis=2).T
    outgoing = jnp.dot(dispatch_map, normed, preferred_element_type=jnp.float32).astype(
        jnp.bfloat16
    )
    outgoing = outgoing.reshape(expert_count, 1, capacity, width)
    outgoing = jnp.broadcast_to(outgoing, (expert_count, 2, capacity, width)).reshape(
        2 * expert_count, capacity, width
    )
    returned = expert_block(
        lax.all_to_all(outgoing, "expert", split_axis=0, concat_axis=0, tiled=True),
        gate_up=gate_up,
        down_proj=down_proj,
    )
    halves = returned.reshape(expert_count, 2, capacity, width).astype(jnp.float32)
    expert_weighted_total = halves[:, 0] + halves[:, 1]
    branch = jnp.dot(
        combine_map,
        expert_weighted_total.reshape(slot_count, width),
        precision=lax.Precision.HIGHEST,
    )
    carried = jnp.einsum("tji,tid->tjd", stream_mixer, widened, precision=lax.Precision.HIGHEST)
    return (carried + post_weight[:, :, None] * branch[:, None, :]).astype(jnp.bfloat16)


def body(paths_in, path_proj, coef_bias, norm_gain, w_gate_up, w_down, routes, route_gate):
    section_index = lax.axis_index("section")
    section_count = lax.axis_size("section")
    micro_count = paths_in.shape[0]
    gate_up = w_gate_up[0, 0].reshape(w_gate_up.shape[2], -1)
    down_proj = w_down[0, 0]
    incoming = jnp.zeros(paths_in.shape[1:], jnp.bfloat16)
    results = jnp.zeros(paths_in.shape, jnp.bfloat16)
    slot_index = jnp.arange(micro_count, dtype=jnp.int32)
    total_steps = micro_count + section_count - 1
    for time_step in range(total_steps):
        micro_index = time_step - section_index
        clipped = jnp.clip(micro_index, 0, micro_count - 1)
        entering = lax.dynamic_index_in_dim(paths_in, clipped, 0, keepdims=False)
        current = jnp.where(section_index == 0, entering, incoming)
        routes_now = lax.dynamic_index_in_dim(routes[0], clipped, 0, keepdims=False)
        gates_now = lax.dynamic_index_in_dim(route_gate[0], clipped, 0, keepdims=False)
        leaving = mix_layer(
            current,
            path_proj[0],
            coef_bias[0],
            norm_gain[0],
            gate_up,
            down_proj,
            routes_now,
            gates_now,
        )
        results = jnp.where(
            (slot_index == micro_index)[:, None, None, None], leaving[None], results
        )
        if time_step + 1 < total_steps:
            incoming = passed_along(leaving, "section", 1)
    return results[None]


def solution(mesh):
    in_specs = (
        P(None, "expert", None, "dp"),
        P("section", None, None, "dp"),
        P("section", None),
        P("section", "dp"),
        P("section", "expert", "dp", None, None),
        P("section", "expert", None, "dp"),
        P("section", None, "expert", None),
        P("section", None, "expert", None),
    )
    out_specs = P("section", None, "expert", None, "dp")
    return jax.shard_map(body, mesh=mesh, in_specs=in_specs, out_specs=out_specs, check_vma=False)
```

profile of v0, /device:TPU:0, one launch (start us, length us, event | category | flops | bytes accessed | tf_op | source)
XLA Modules:
  0.0 375.9 jit_solution(183301139221659460)
XLA Ops:
  10.1 15.1 %all-reduce.2 = (f32[64,24]{0,1:T(8,128)S(1)}, f32[64]{0:T(128)S(1)}, f32[64,4,4]{2,1,0:T(4,128)}) all-reduce(f32[64,24]{0,1:T(8,128)S(1)} %convolution_bitcast_fusion.2, f32[64]{0:T(128)S(1)} %get-tuple-element.18, f32[64,4,4]{2,1,0:T(4,128)S(1)} %fusion.129), channel_id=1, replica_groups=mesh['dp'=4,'section'=2,'expert'=4] {'dp'}, use_global_device_ids=true, to_apply=%region_0.1 | all-reduce | flops 2624 | bytes 20992 | tf_op jit(solution)/shard_map/psum | solution.py:45
  40.5 4.9 %all-to-all-start = ((bf16[4,32,1792]{2,1,0:T(8,128)(2,1)}), bf16[4,32,1792]{2,1,0:T(8,128)(2,1)S(1)}, u32[]{:S(2)}, u32[]{:S(2)}) async-start(bf16[4,32,1792]{2,1,0:T(8,128)(2,1)} %bitcast.125), calls=%async_computation | async-start | bytes 917504 | tf_op jit(solution)/shard_map/all_to_all | solution.py:91
  58.4 4.8 %copy.306 = bf16[224,8,2,512]{3,1,2,0:T(8,128)(2,1)} copy(bf16[224,8,2,512]{3,2,1,0:T(2,128)(2,1)} %bitcast.121) | data formatting | bytes 7340032
  64.5 3.5 fusion.266
  70.8 31.3 %all-reduce.7.cloned.1.call-done = f32[128,1024]{1,0:T(8,128)} async-done(((f32[128,1024]{1,0:T(8,128)}), f32[128,1024]{1,0:T(8,128)}) %all-reduce.7.cloned.1.call-update) | async-done | bytes 524304 | tf_op jit(solution)/shard_map/psum | solution.py:32
  104.4 4.6 %all-to-all-start.1 = ((bf16[4,32,1792]{2,1,0:T(8,128)(2,1)}), bf16[4,32,1792]{2,1,0:T(8,128)(2,1)S(1)}, u32[]{:S(2)}, u32[]{:S(2)}) async-start(bf16[4,32,1792]{2,1,0:T(8,128)(2,1)} %bitcast.139), calls=%async_computation.1 | async-start | bytes 917504 | tf_op jit(solution)/shard_map/all_to_all | solution.py:36
  116.1 5.1 %all-to-all-done.1 = bf16[4,32,1792]{2,1,0:T(8,128)(2,1)S(1)} async-done(((bf16[4,32,1792]{2,1,0:T(8,128)(2,1)}), bf16[4,32,1792]{2,1,0:T(8,128)(2,1)S(1)}, u32[]{:S(2)}, u32[]{:S(2)}) %all-to-all-start.1) | async-done | bytes 458784 | tf_op jit(solution)/shard_map/all_to_all | solution.py:36
  125.6 4.3 %collective-permute-start = (bf16[64,4,1792]{2,1,0:T(4,128)(2,1)}, bf16[64,4,1792]{2,1,0:T(4,128)(2,1)}, u32[]{:S(2)}, u32[]{:S(2)}) collective-permute-start(bf16[64,4,1792]{2,1,0:T(4,128)(2,1)} %fusion.57), channel_id=1, source_target_pairs={{0,4},{1,5},{2,6},{3,7},{8,12},{9,13},{10,14},{11,15},{16,20},{17,... | collective-permute-start | bytes 2752520 | tf_op jit(solution)/shard_map/ppermute | solution.py:17
  130.9 17.1 %collective-permute-done = bf16[64,4,1792]{2,1,0:T(4,128)(2,1)} collective-permute-done((bf16[64,4,1792]{2,1,0:T(4,128)(2,1)}, bf16[64,4,1792]{2,1,0:T(4,128)(2,1)}, u32[]{:S(2)}, u32[]{:S(2)}) %collective-permute-start) | collective-permute-done | bytes 917536 | tf_op jit(solution)/shard_map/ppermute | solution.py:17
  152.1 11.8 %all-reduce.1 = (f32[64,24]{0,1:T(8,128)S(1)}, f32[64]{0:T(128)S(1)}, f32[64,4,4]{2,1,0:T(4,128)S(1)}) all-reduce(f32[64,24]{0,1:T(8,128)S(1)} %convolution_bitcast_fusion.1, f32[64]{0:T(128)S(1)} %get-tuple-element.16, f32[64,4,4]{2,1,0:T(4,128)S(1)} %fusion.267), channel_id=1, replica_groups=mesh['dp'=4,'section'=2,'expert'=4] {'dp'}, use_global_device_ids=true, to_apply=%region_48.49 | all-reduce | flops 2624 | bytes 20992 | tf_op jit(solution)/shard_map/psum | solution.py:45
  168.5 3.5 all-to-all-start.2
  185.8 3.5 fusion.269
  192.1 33.4 %all-reduce.9.cloned.1.call-done = f32[128,1024]{1,0:T(8,128)} async-done(((f32[128,1024]{1,0:T(8,128)}), f32[128,1024]{1,0:T(8,128)}) %all-reduce.9.cloned.1.call-update) | async-done | bytes 524304 | tf_op jit(solution)/shard_map/psum | solution.py:32
  227.8 4.6 %all-to-all-start.3 = ((bf16[4,32,1792]{2,1,0:T(8,128)(2,1)}), bf16[4,32,1792]{2,1,0:T(8,128)(2,1)S(1)}, u32[]{:S(2)}, u32[]{:S(2)}) async-start(bf16[4,32,1792]{2,1,0:T(8,128)(2,1)} %bitcast.137), calls=%async_computation.3 | async-start | bytes 917504 | tf_op jit(solution)/shard_map/all_to_all | solution.py:36
  239.0 5.6 %all-to-all-done.3 = bf16[4,32,1792]{2,1,0:T(8,128)(2,1)S(1)} async-done(((bf16[4,32,1792]{2,1,0:T(8,128)(2,1)}), bf16[4,32,1792]{2,1,0:T(8,128)(2,1)S(1)}, u32[]{:S(2)}, u32[]{:S(2)}) %all-to-all-start.3) | async-done | bytes 458784 | tf_op jit(solution)/shard_map/all_to_all | solution.py:36
  248.8 4.3 %collective-permute-start.1 = (bf16[64,4,1792]{2,1,0:T(4,128)(2,1)}, bf16[64,4,1792]{2,1,0:T(4,128)(2,1)}, u32[]{:S(2)}, u32[]{:S(2)}) collective-permute-start(bf16[64,4,1792]{2,1,0:T(4,128)(2,1)} %fusion.58), channel_id=1, source_target_pairs={{0,4},{1,5},{2,6},{3,7},{8,12},{9,13},{10,14},{11,15},{16,20},{17,... | collective-permute-start | bytes 2752520 | tf_op jit(solution)/shard_map/ppermute | solution.py:17
  255.0 16.2 %collective-permute-done.1 = bf16[64,4,1792]{2,1,0:T(4,128)(2,1)} collective-permute-done((bf16[64,4,1792]{2,1,0:T(4,128)(2,1)}, bf16[64,4,1792]{2,1,0:T(4,128)(2,1)}, u32[]{:S(2)}, u32[]{:S(2)}) %collective-permute-start.1) | collective-permute-done | bytes 917536 | tf_op jit(solution)/shard_map/ppermute | solution.py:17
  275.3 11.8 %all-reduce = (f32[64,24]{0,1:T(8,128)S(1)}, f32[64]{0:T(128)S(1)}, f32[64,4,4]{2,1,0:T(4,128)S(1)}) all-reduce(f32[64,24]{0,1:T(8,128)S(1)} %convolution_bitcast_fusion, f32[64]{0:T(128)S(1)} %get-tuple-element.14, f32[64,4,4]{2,1,0:T(4,128)S(1)} %fusion.270), channel_id=1, replica_groups=mesh['dp'=4,'section'=2,'expert'=4] {'dp'}, use_global_device_ids=true, to_apply=%region_96.97 | all-reduce | flops 2624 | bytes 20992 | tf_op jit(solution)/shard_map/psum | solution.py:45
  290.6 3.5 all-to-all-start.4
  294.7 13.0 %all-to-all-done.4 = bf16[4,32,1792]{2,1,0:T(8,128)(2,1)S(1)} async-done(((bf16[4,32,1792]{2,1,0:T(8,128)(2,1)}), bf16[4,32,1792]{2,1,0:T(8,128)(2,1)S(1)}, u32[]{:S(2)}, u32[]{:S(2)}) %all-to-all-start.4) | async-done | bytes 458784 | tf_op jit(solution)/shard_map/all_to_all | solution.py:91
  307.6 3.5 fusion.272
  311.2 32.9 %all-reduce.11.cloned.1.call-done = f32[128,1024]{1,0:T(8,128)} async-done(((f32[128,1024]{1,0:T(8,128)}), f32[128,1024]{1,0:T(8,128)}) %all-reduce.11.cloned.1.call-update) | async-done | bytes 524304 | tf_op jit(solution)/shard_map/psum | solution.py:32
  346.4 4.6 %all-to-all-start.5 = ((bf16[4,32,1792]{2,1,0:T(8,128)(2,1)}), bf16[4,32,1792]{2,1,0:T(8,128)(2,1)S(1)}, u32[]{:S(2)}, u32[]{:S(2)}) async-start(bf16[4,32,1792]{2,1,0:T(8,128)(2,1)} %bitcast.138), calls=%async_computation.5 | async-start | bytes 917504 | tf_op jit(solution)/shard_map/all_to_all | solution.py:36
  351.3 11.8 %all-to-all-done.5 = bf16[4,32,1792]{2,1,0:T(8,128)(2,1)S(1)} async-done(((bf16[4,32,1792]{2,1,0:T(8,128)(2,1)}), bf16[4,32,1792]{2,1,0:T(8,128)(2,1)S(1)}, u32[]{:S(2)}, u32[]{:S(2)}) %all-to-all-start.5) | async-done | bytes 458784 | tf_op jit(solution)/shard_map/all_to_all | solution.py:36
  (228 shorter events, 107.5 us)
Async XLA Ops:
  6.5 95.6 %copy-start = (bf16[1,1,512,1792]{3,2,1,0:T(8,128)(2,1)S(1)}, bf16[1,1,512,1792]{3,2,1,0:T(8,128)(2,1)}, u32[]{:S(2)}) copy-start(bf16[1,1,512,1792]{3,2,1,0:T(8,128)(2,1)} %param.13) | copy-start | bytes 5505028
  8.5 16.7 %copy-start.18 = (f32[1,24]{1,0:T(1,128)S(1)}, f32[1,24]{1,0:T(1,128)}, u32[]{:S(2)}) copy-start(f32[1,24]{1,0:T(1,128)} %param.10) | copy-start | bytes 292
  40.5 24.0 %all-to-all-start = ((bf16[4,32,1792]{2,1,0:T(8,128)(2,1)}), bf16[4,32,1792]{2,1,0:T(8,128)(2,1)S(1)}, u32[]{:S(2)}, u32[]{:S(2)}) async-start(bf16[4,32,1792]{2,1,0:T(8,128)(2,1)} %bitcast.125), calls=%async_computation | async-start | bytes 917504 | tf_op jit(solution)/shard_map/all_to_all | solution.py:91
  45.4 56.8 %all-reduce.7.cloned.1.call-start = ((), (), s32[]{:S(2)}) async-start(), calls=%async_computation.6 | async-start | bytes 1048576 | tf_op jit(solution)/shard_map/psum | solution.py:32
  104.4 16.7 %all-to-all-start.1 = ((bf16[4,32,1792]{2,1,0:T(8,128)(2,1)}), bf16[4,32,1792]{2,1,0:T(8,128)(2,1)S(1)}, u32[]{:S(2)}, u32[]{:S(2)}) async-start(bf16[4,32,1792]{2,1,0:T(8,128)(2,1)} %bitcast.139), calls=%async_computation.1 | async-start | bytes 917504 | tf_op jit(solution)/shard_map/all_to_all | solution.py:36
  122.4 7.5 %copy-start.14 = (s32[64]{0:T(128)S(1)}, s32[64]{0:T(128)}, u32[]{:S(2)}) copy-start(s32[64]{0:T(128)} %get-tuple-element.29) | copy-start | bytes 772
  125.6 22.4 %collective-permute-start = (bf16[64,4,1792]{2,1,0:T(4,128)(2,1)}, bf16[64,4,1792]{2,1,0:T(4,128)(2,1)}, u32[]{:S(2)}, u32[]{:S(2)}) collective-permute-start(bf16[64,4,1792]{2,1,0:T(4,128)(2,1)} %fusion.57), channel_id=1, source_target_pairs={{0,4},{1,5},{2,6},{3,7},{8,12},{9,13},{10,14},{11,15},{16,20},{17,... | collective-permute-start | bytes 2752520 | tf_op jit(solution)/shard_map/ppermute | solution.py:17
  130.9 36.5 %copy-start.26 = (s32[64]{0:T(128)}, s32[64]{0:T(128)S(1)}, u32[]{:S(2)}) copy-start(s32[64]{0:T(128)S(1)} %multiply_add_fusion.4) | copy-start | bytes 772
  150.6 13.2 %copy-start.19 = (f32[1,24]{1,0:T(1,128)S(1)}, f32[1,24]{1,0:T(1,128)}, u32[]{:S(2)}) copy-start(f32[1,24]{1,0:T(1,128)} %param.10) | copy-start | bytes 292
  151.7 15.7 %copy-start.3 = (f32[1792]{0:T(1024)S(1)}, f32[1792]{0:T(1024)}, u32[]{:S(2)}) copy-start(f32[1792]{0:T(1024)} %copy-done.2) | copy-start | bytes 21508
  168.5 17.3 %all-to-all-start.2 = ((bf16[4,32,1792]{2,1,0:T(8,128)(2,1)}), bf16[4,32,1792]{2,1,0:T(8,128)(2,1)S(1)}, u32[]{:S(2)}, u32[]{:S(2)}) async-start(bf16[4,32,1792]{2,1,0:T(8,128)(2,1)} %bitcast.127), calls=%async_computation.2 | async-start | bytes 917504 | tf_op jit(solution)/shard_map/all_to_all | solution.py:91
  172.0 53.6 %all-reduce.9.cloned.1.call-start = ((), (), s32[]{:S(2)}) async-start(), calls=%async_computation.7 | async-start | bytes 1048576 | tf_op jit(solution)/shard_map/psum | solution.py:32
  173.3 11.3 %copy-start.5 = (f32[64,16]{0,1:T(8,128)S(1)}, f32[64,16]{0,1:T(8,128)}, u32[]{:S(2)}) copy-start(f32[64,16]{0,1:T(8,128)} %slice_exponential_fusion.1) | copy-start | bytes 12292
  227.8 16.7 %all-to-all-start.3 = ((bf16[4,32,1792]{2,1,0:T(8,128)(2,1)}), bf16[4,32,1792]{2,1,0:T(8,128)(2,1)S(1)}, u32[]{:S(2)}, u32[]{:S(2)}) async-start(bf16[4,32,1792]{2,1,0:T(8,128)(2,1)} %bitcast.137), calls=%async_computation.3 | async-start | bytes 917504 | tf_op jit(solution)/shard_map/all_to_all | solution.py:36
  245.8 9.0 %copy-start.15 = (s32[64]{0:T(128)S(1)}, s32[64]{0:T(128)}, u32[]{:S(2)}) copy-start(s32[64]{0:T(128)} %get-tuple-element.29) | copy-start | bytes 772
  248.8 22.4 %collective-permute-start.1 = (bf16[64,4,1792]{2,1,0:T(4,128)(2,1)}, bf16[64,4,1792]{2,1,0:T(4,128)(2,1)}, u32[]{:S(2)}, u32[]{:S(2)}) collective-permute-start(bf16[64,4,1792]{2,1,0:T(4,128)(2,1)} %fusion.58), channel_id=1, source_target_pairs={{0,4},{1,5},{2,6},{3,7},{8,12},{9,13},{10,14},{11,15},{16,20},{17,... | collective-permute-start | bytes 2752520 | tf_op jit(solution)/shard_map/ppermute | solution.py:17
  255.0 34.4 %copy-start.24 = (s32[64]{0:T(128)}, s32[64]{0:T(128)S(1)}, u32[]{:S(2)}) copy-start(s32[64]{0:T(128)S(1)} %multiply_add_fusion.3) | copy-start | bytes 772
  273.8 13.3 %copy-start.20 = (f32[1,24]{1,0:T(1,128)S(1)}, f32[1,24]{1,0:T(1,128)}, u32[]{:S(2)}) copy-start(f32[1,24]{1,0:T(1,128)} %param.10) | copy-start | bytes 292
  274.9 14.6 %copy-start.4 = (f32[1792]{0:T(1024)S(1)}, f32[1792]{0:T(1024)}, u32[]{:S(2)}) copy-start(f32[1792]{0:T(1024)} %copy-done.2) | copy-start | bytes 21508
  290.6 17.1 %all-to-all-start.4 = ((bf16[4,32,1792]{2,1,0:T(8,128)(2,1)}), bf16[4,32,1792]{2,1,0:T(8,128)(2,1)S(1)}, u32[]{:S(2)}, u32[]{:S(2)}) async-start(bf16[4,32,1792]{2,1,0:T(8,128)(2,1)} %bitcast.126), calls=%async_computation.4 | async-start | bytes 917504 | tf_op jit(solution)/shard_map/all_to_all | solution.py:91
  294.0 50.1 %all-reduce.11.cloned.1.call-start = ((), (), s32[]{:S(2)}) async-start(), calls=%async_computation.8 | async-start | bytes 1048576 | tf_op jit(solution)/shard_map/psum | solution.py:32
  346.4 16.7 %all-to-all-start.5 = ((bf16[4,32,1792]{2,1,0:T(8,128)(2,1)}), bf16[4,32,1792]{2,1,0:T(8,128)(2,1)S(1)}, u32[]{:S(2)}, u32[]{:S(2)}) async-start(bf16[4,32,1792]{2,1,0:T(8,128)(2,1)} %bitcast.138), calls=%async_computation.5 | async-start | bytes 917504 | tf_op jit(solution)/shard_map/all_to_all | solution.py:36
  351.0 12.3 %copy-start.21 = (f32[64]{0:T(128)S(1)}, f32[64]{0:T(128)}, u32[]{:S(2)}) copy-start(f32[64]{0:T(128)} %get-tuple-element.26) | copy-start | bytes 772
  351.0 12.3 %copy-start.25 = (s32[64]{0:T(128)S(1)}, s32[64]{0:T(128)}, u32[]{:S(2)}) copy-start(s32[64]{0:T(128)} %copy-done.24) | copy-start | bytes 772
  (20 other events, 39.2 us)
Sparse Core Ops, SparseCore 0:
  68.2 33.9 all-reduce.6
  189.4 36.0 all-reduce.8
  311.3 32.8 all-reduce.10
where the time goes:
time: 380 us; the launch traced here: 376 us
  waiting for transfers between devices  166 us (44%)
  other arithmetic  63.2 us (17%)
  blocking collectives  38.8 us (10%)
  matrix products  35.5 us (9%)
  starting transfers between devices  34.3 us (9%)
  local copies, waits for them, and re-layouts  23.9 us (6%)
  between operations  13.8 us (4%)
    psum x3, waiting for transfers between devices, expert_block(): summed = lax.psum(hidden_pre, 'dp')  97.7 us
    psum x3, blocking collectives, mix_layer(): lax.psum((square_part, projected, path_gram), 'dp')  38.8 us
    ppermute x2, waiting for transfers between devices, passed_along(): lax.ppermute(value, axis, [(source, source + steps) for source in range(l...  33.3 us
    div x57, other arithmetic, doubly_stochastic_project(): stream_mixer = stream_mixer / jnp.sum(stream_mixer, axis=2, keepdims=True)  33 us
    all_to_all x3, waiting for transfers between devices, expert_block(): lax.all_to_all(expert_output_rows, 'expert', split_axis=0, concat_axis=0,...  22.4 us
    all_to_all x3, starting transfers between devices, expert_block(): lax.all_to_all(expert_output_rows, 'expert', split_axis=0, concat_axis=0,...  13.8 us
    all_to_all x3, waiting for transfers between devices, mix_layer(): lax.all_to_all(outgoing, 'expert', split_axis=0, concat_axis=0, tiled=True)  13 us
    all_to_all x3, starting transfers between devices, mix_layer(): lax.all_to_all(outgoing, 'expert', split_axis=0, concat_axis=0, tiled=True)  11.8 us
  transfers between devices with their start and end apart: 11, of which 9 were waited for; matrix products, arithmetic and copies ran while one was open for 15% of the time, Pallas kernels for 0%

commit v1 on v0

v1 whole, which is shorter than its diff:
```python
import functools

import jax
import jax.numpy as jnp
from jax import lax
from jax.experimental import pallas as pl
from jax.experimental.pallas import tpu as pltpu
from jax.sharding import PartitionSpec as P

SINK = 20
EPSILON = 1e-06
MESH = pl.DeviceIdType.MESH
F32 = jnp.float32
BF16 = jnp.bfloat16
LANES = 128
NT = (((1,), (1,)), ((), ()))


def kernel(
    sizes,
    paths_ref, proj_ref, bias_ref, gain_ref, gate_up_ref, down_ref, routes_ref, gates_ref,
    out_ref,
    path, wgu, wd, stats, crow, tab, slotcol, outgoing, recv, acc, part, rs_recv, hid, half_out, ret,
    branch, acc_branch, in_crow, in_branch, obuf,
    load_sem, out_sem, st_s, st_r, di_s, di_r, rs_s, rs_r, ag_s, ag_r, re_s, re_r, se_s, se_r,
):
    micro, streams, rows, width, coefs, inner, cap, n_dp, n_ex, n_sec, depth = sizes
    experts = n_ex // 2
    slots = experts * cap
    items = n_ex * cap
    share = items // n_dp
    shift = cap.bit_length() - 1
    dp, ex, sec = (lax.axis_index(a) for a in ("dp", "expert", "section"))
    pre0, post0, scale0, mix0 = 0, streams, 2 * streams, 2 * streams + 1

    barrier = pltpu.get_barrier_semaphore()
    greeted = 0
    for name, me, count in (("dp", dp, n_dp), ("expert", ex, n_ex), ("section", sec, n_sec)):
        for off in range(1, count):
            pl.semaphore_signal(
                barrier, inc=1, device_id={name: lax.rem(me + off, count)}, device_id_type=MESH
            )
            greeted += 1

    loads = [
        pltpu.make_async_copy(paths_ref.at[m], path.at[m], load_sem.at[m]) for m in range(micro)
    ]
    load_gu = pltpu.make_async_copy(gate_up_ref, wgu, load_sem.at[micro])
    load_d = pltpu.make_async_copy(down_ref, wd, load_sem.at[micro + 1])
    for c in (*loads, load_gu, load_d):
        c.start()

    def remote(src, dst, send, receive, name, target):
        return pltpu.make_async_remote_copy(
            src_ref=src, dst_ref=dst, send_sem=send, recv_sem=receive,
            device_id={name: target}, device_id_type=MESH,
        )

    eye = lax.broadcasted_iota(jnp.int32, (rows, rows), 0) == lax.broadcasted_iota(
        jnp.int32, (rows, rows), 1
    )
    below = (
        lax.broadcasted_iota(jnp.int32, (rows, rows), 1)
        < lax.broadcasted_iota(jnp.int32, (rows, rows), 0)
    )

    def columns(table_ref, first, last):
        turned = jnp.transpose(table_ref[...])
        for k in range(first, last):
            tab[k] = jnp.broadcast_to(turned[:rows, k : k + 1], (rows, LANES))

    def mixed(m, c, added):
        cols = pl.ds(pl.multiple_of(c * LANES, LANES), LANES)
        p = [path[m, i, :, cols].astype(F32) for i in range(streams)]
        res = []
        for j in range(streams):
            total = tab[post0 + j] * added(cols)
            for i in range(streams):
                total = total + tab[mix0 + j * streams + i] * p[i]
            res.append(total.astype(BF16))
        return cols, res

    def stage_stats(m):
        loads[m].wait()
        for layer in range(n_sec - 1):
            @pl.when(sec > layer)
            def _():
                remote(crow.at[m], in_crow.at[m, layer], se_s.at[m, 0, 0],
                       se_r.at[m, layer, 0], "section", layer).wait_recv()
                columns(in_crow.at[m, layer], post0, mix0 + streams * streams)
                remote(branch.at[m], in_branch.at[m, layer], se_s.at[m, 0, 1],
                       se_r.at[m, layer, 1], "section", layer).wait_recv()

                @pl.loop(0, width // LANES)
                def _(c):
                    cols, res = mixed(m, c, lambda s: in_branch[m, layer, :, s].astype(F32))
                    for j in range(streams):
                        path[m, j, :, cols] = res[j]

        projected = jnp.zeros((coefs, rows), F32)
        at = coefs
        for j in range(streams):
            pj = path[m, j]
            projected = projected + lax.dot_general(
                proj_ref[j], pj, NT, preferred_element_type=F32
            )
            for i in range(j + 1):
                g = lax.dot_general(path[m, i], pj, NT, preferred_element_type=F32)
                stats[m, dp, at : at + 1, :] = jnp.sum(jnp.where(eye, g, 0.0), axis=0, keepdims=True)
                at += 1
        stats[m, dp, :coefs, :] = projected
        if m == 0:
            pl.semaphore_wait(barrier, greeted)
        return [
            remote(stats.at[m, dp], stats.at[m, dp], st_s.at[m, off - 1], st_r.at[m, off - 1],
                   "dp", lax.rem(dp + off, n_dp))
            for off in range(1, n_dp)
        ]

    def await_from(m, buf, sems, name, me, count):
        for off in range(1, count):
            source = lax.rem(me + count - off, count)
            remote(buf.at[m, source], buf.at[m, source], sems[0].at[m, off - 1],
                   sems[1].at[m, off - 1], name, source).wait_recv()

    def stage_dispatch(m):
        await_from(m, stats, (st_s, st_r), "dp", dp, n_dp)
        total = stats[m, 0]
        for d in range(1, n_dp):
            total = total + stats[m, d]
        gram, at = {}, coefs
        for j in range(streams):
            for i in range(j + 1):
                gram[i, j] = total[at : at + 1]
                at += 1
        square = gram[0, 0]
        for i in range(1, streams):
            square = square + gram[i, i]
        bias_eye = lax.broadcasted_iota(jnp.int32, (coefs, coefs), 0) == lax.broadcasted_iota(
            jnp.int32, (coefs, coefs), 1
        )
        bias = jnp.sum(jnp.where(bias_eye, bias_ref[...], 0.0), axis=1, keepdims=True)
        logits = total[:coefs] * lax.rsqrt(square * (1.0 / (streams * depth)) + EPSILON) + bias
        weights = jax.nn.sigmoid(logits[: 2 * streams])
        crow[m, pre0:streams, :rows] = weights[:streams]
        crow[m, post0 : 2 * streams, :rows] = 2.0 * weights[streams:]
        norm = jnp.zeros_like(square)
        for i, j in gram:
            pair = weights[i : i + 1] * weights[j : j + 1] * gram[i, j]
            norm = norm + (pair if i == j else 2.0 * pair)
        crow[m, scale0 : scale0 + 1, :rows] = lax.rsqrt(norm * (1.0 / depth) + EPSILON)
        columns(crow.at[m], pre0, scale0 + 1)

        route = routes_ref[m]
        lane = lax.broadcasted_iota(jnp.int32, (rows, LANES), 1)
        chosen = (lane == route).astype(F32)
        earlier = jnp.dot(
            below.astype(F32).astype(BF16), chosen.astype(BF16), preferred_element_type=F32
        )
        rank = jnp.sum(earlier * chosen, axis=1, keepdims=True)
        slot = route.astype(F32) * cap + rank
        slotcol[m] = slot
        slotrow = jnp.sum(jnp.where(eye, slot, 0.0), axis=0, keepdims=True)
        pick = (
            lax.broadcasted_iota(jnp.int32, (slots, rows), 0).astype(F32) == slotrow
        ).astype(F32).astype(BF16)

        @pl.loop(0, width // LANES)
        def _(c):
            cols = pl.ds(pl.multiple_of(c * LANES, LANES), LANES)
            merged = tab[pre0] * path[m, 0, :, cols].astype(F32)
            for i in range(1, streams):
                merged = merged + tab[pre0 + i] * path[m, i, :, cols].astype(F32)
            normed = (merged * tab[scale0] * gain_ref[:, cols].astype(F32)).astype(BF16)
            moved = jnp.dot(pick, normed, preferred_element_type=F32).astype(BF16)
            outgoing[m, :, :, cols] = moved.reshape(experts, cap, LANES)

        copies = []
        for off in range(1, n_ex):
            target = lax.rem(ex + off, n_ex)
            copies.append(
                remote(outgoing.at[m, lax.div(target, 2)], recv.at[m, ex], di_s.at[m, off - 1],
                       di_r.at[m, off - 1], "expert", target)
            )
            copies[-1].start()
        recv[m, ex] = outgoing[m, lax.div(ex, 2)]

        start = jnp.exp(logits[2 * streams :])
        entries = tuple(start[k : k + 1] for k in range(streams * streams))

        def balance(_, a):
            a = list(a)
            for groups in (
                [[j * streams + i for i in range(streams)] for j in range(streams)],
                [[j * streams + i for j in range(streams)] for i in range(streams)],
            ):
                for group in groups:
                    inverse = 1.0 / functools.reduce(jnp.add, [a[k] for k in group])
                    for k in group:
                        a[k] = a[k] * inverse
            return tuple(a)

        entries = lax.fori_loop(0, SINK, balance, entries)
        for k in range(streams * streams):
            crow[m, mix0 + k : mix0 + k + 1, :rows] = entries[k]
        to_sections(m, crow, in_crow, 0, "start")
        return copies

    def to_sections(m, src, dst, kind, act):
        for off in range(1, n_sec):
            @pl.when(sec + off < n_sec)
            def _():
                copy = remote(src.at[m], dst.at[m, sec], se_s.at[m, off - 1, kind],
                              se_r.at[m, sec, kind], "section", sec + off)
                copy.start() if act == "start" else copy.wait_send()

    def stage_up(m):
        await_from(m, recv, (di_s, di_r), "expert", ex, n_ex)
        if m == 0:
            load_gu.wait()
        tile = 256

        @pl.loop(0, 2 * inner // tile)
        def _(c):
            cols = pl.ds(pl.multiple_of(c * tile, tile), tile)
            product = jnp.dot(
                recv[m].reshape(items, width), wgu[:, cols], preferred_element_type=F32
            )
            acc[m, :, :, cols] = product.reshape(n_dp, share, tile)
            part[m, :, :, cols] = product.astype(BF16).reshape(n_dp, share, tile)

        return [
            remote(part.at[m, lax.rem(dp + off, n_dp)], rs_recv.at[m, off - 1],
                   rs_s.at[m, off - 1], rs_r.at[m, off - 1], "dp", lax.rem(dp + off, n_dp))
            for off in range(1, n_dp)
        ]

    def stage_hidden(m):
        for off in range(1, n_dp):
            remote(part.at[m, 0], rs_recv.at[m, off - 1], rs_s.at[m, off - 1],
                   rs_r.at[m, off - 1], "dp", lax.rem(dp + off, n_dp)).wait_recv()
        total = acc[m, dp]
        for off in range(1, n_dp):
            total = total + rs_recv[m, off - 1].astype(F32)
        gate = total[:, :inner]
        hid[m, dp] = (gate * jax.nn.sigmoid(gate) * total[:, inner:]).astype(BF16)
        return [
            remote(hid.at[m, dp], hid.at[m, dp], ag_s.at[m, off - 1], ag_r.at[m, off - 1],
                   "dp", lax.rem(dp + off, n_dp))
            for off in range(1, n_dp)
        ]

    def stage_down(m):
        await_from(m, hid, (ag_s, ag_r), "dp", dp, n_dp)
        if m == 0:
            load_d.wait()
        tile = 256 if width % 256 == 0 else LANES

        @pl.loop(0, width // tile)
        def _(c):
            cols = pl.ds(pl.multiple_of(c * tile, tile), tile)
            product = jnp.dot(
                hid[m].reshape(items, inner), wd[:, cols], preferred_element_type=F32
            )
            half_out[m, :, :, cols] = product.astype(BF16).reshape(n_ex, cap, tile)

        copies = [
            remote(half_out.at[m, lax.rem(ex + off, n_ex)], ret.at[m, ex], re_s.at[m, off - 1],
                   re_r.at[m, off - 1], "expert", lax.rem(ex + off, n_ex))
            for off in range(1, n_ex)
        ]
        for copy in copies:
            copy.start()
        ret[m, ex] = half_out[m, ex]
        return copies

    def stage_combine(m):
        columns(crow.at[m], post0, mix0 + streams * streams)
        place = lax.broadcasted_iota(jnp.int32, (rows, items), 1)
        place = ((place >> (shift + 1)) << shift) + (place & (cap - 1))
        back = (place.astype(F32) == slotcol[m]).astype(F32).astype(BF16)
        gates = gates_ref[m]
        await_from(m, ret, (re_s, re_r), "expert", ex, n_ex)
        tile = 256 if width % 256 == 0 else LANES

        @pl.loop(0, width // tile)
        def _(c):
            cols = pl.ds(pl.multiple_of(c * tile, tile), tile)
            value = gates * jnp.dot(
                back, ret[m, :, :, cols].reshape(items, tile), preferred_element_type=F32
            )
            acc_branch[:, cols] = value
            branch[m, :, cols] = value.astype(BF16)

        to_sections(m, branch, in_branch, 1, "start")

        @pl.loop(0, width // LANES)
        def _(c):
            cols, res = mixed(m, c, lambda s: acc_branch[:, s])
            for j in range(streams):
                obuf[m, j, :, cols] = res[j]

        pltpu.make_async_copy(obuf.at[m], out_ref.at[m], out_sem.at[m]).start()
        return []

    stages = (stage_stats, stage_dispatch, stage_up, stage_hidden, stage_down, stage_combine)
    crow[...] = jnp.zeros_like(crow)
    order = sorted(
        ((step + m, m, step) for m in range(micro) for step in range(len(stages)))
    )
    sent = []
    for _, m, step in order:
        copies = stages[step](m)
        if step not in (1, 4):
            for copy in copies:
                copy.start()
        sent += copies
    for copy in sent:
        copy.wait_send()
    for m in range(micro):
        to_sections(m, crow, in_crow, 0, "wait")
        to_sections(m, branch, in_branch, 1, "wait")
        pltpu.make_async_copy(obuf.at[m], out_ref.at[m], out_sem.at[m]).wait()


def body(paths_in, path_proj, coef_bias, norm_gain, w_gate_up, w_down, routes, route_gate):
    n_dp, n_ex, n_sec = (lax.axis_size(a) for a in ("dp", "expert", "section"))
    micro, rows, streams, width = paths_in.shape
    coefs, inner = path_proj.shape[1], w_down.shape[2]
    experts = n_ex // 2
    need = min(rows, max(2, -(-rows // experts)))
    cap = 16
    while cap < need:
        cap *= 2
    items, later = n_ex * cap, max(1, n_sec - 1)
    share = items // n_dp
    pairs = streams * (streams + 1) // 2
    stat_rows = -(-(coefs + pairs) // 8) * 8
    table = 2 * streams + 1 + streams * streams
    table_rows = -(-table // 8) * 8
    sizes = (micro, streams, rows, width, coefs, inner, cap, n_dp, n_ex, n_sec, width * n_dp)
    vmem, dma = pltpu.VMEM, pltpu.SemaphoreType.DMA
    scratch = [
        vmem((micro, streams, rows, width), BF16),
        vmem((width, 2 * inner), BF16),
        vmem((inner, width), BF16),
        vmem((micro, n_dp, stat_rows, rows), F32),
        vmem((micro, table_rows, LANES), F32),
        vmem((table, rows, LANES), F32),
        vmem((micro, rows, 1), F32),
        vmem((micro, experts, cap, width), BF16),
        vmem((micro, n_ex, cap, width), BF16),
        vmem((micro, n_dp, share, 2 * inner), F32),
        vmem((micro, n_dp, share, 2 * inner), BF16),
        vmem((micro, n_dp - 1, share, 2 * inner), BF16),
        vmem((micro, n_dp, share, inner), BF16),
        vmem((micro, n_ex, cap, width), BF16),
        vmem((micro, n_ex, cap, width), BF16),
        vmem((micro, rows, width), BF16),
        vmem((rows, width), F32),
        vmem((micro, later, table_rows, LANES), F32),
        vmem((micro, later, rows, width), BF16),
        vmem((micro, streams, rows, width), BF16),
        dma((micro + 2,)),
        dma((micro,)),
        *(dma((micro, n - 1)) for n in (n_dp, n_dp, n_ex, n_ex, n_dp, n_dp, n_dp, n_dp, n_ex, n_ex)),
        dma((micro, later, 2)),
        dma((micro, later, 2)),
    ]
    hbm, local = pl.BlockSpec(memory_space=pl.ANY), pl.BlockSpec(memory_space=pltpu.VMEM)
    out = pl.pallas_call(
        functools.partial(kernel, sizes),
        out_shape=jax.ShapeDtypeStruct((micro, streams, rows, width), BF16),
        in_specs=[hbm, local, local, local, hbm, hbm, local, local],
        out_specs=hbm,
        scratch_shapes=scratch,
        compiler_params=pltpu.CompilerParams(collective_id=0, has_side_effects=True),
    )(
        jnp.transpose(paths_in, (0, 2, 1, 3)),
        jnp.transpose(path_proj[0], (1, 0, 2)),
        coef_bias,
        norm_gain,
        w_gate_up[0, 0].reshape(width, -1),
        w_down[0, 0],
        routes[0],
        route_gate[0],
    )
    return jnp.transpose(out, (0, 2, 1, 3))[None]


def solution(mesh):
    in_specs = (
        P(None, "expert", None, "dp"),
        P("section", None, None, "dp"),
        P("section", None),
        P("section", "dp"),
        P("section", "expert", "dp", None, None),
        P("section", "expert", None, "dp"),
        P("section", None, "expert", None),
        P("section", None, "expert", None),
    )
    out_specs = P("section", None, "expert", None, "dp")
    return jax.shard_map(body, mesh=mesh, in_specs=in_specs, out_specs=out_specs, check_vma=False)
```

time: 380 us -> 132 us (0.35)
  the two profiles are of different devices: /device:TPU:0 before, /device:TPU:14 now
where the time goes in v1:
time: 132 us; the launch traced here: 131 us
  Pallas kernels  117 us (89%)
  local copies, waits for them, and re-layouts  14.6 us (11%)
    pallas_call x1, Pallas kernels, body(): pl.pallas_call(functools.partial(kernel, sizes), out_shape=jax.ShapeDtype...  117 us
    unnamed x5, local copies, waits for them, and re-layouts  7.63 us
    broadcast_in_dim x1, local copies, waits for them, and re-layouts, body(): return jnp.transpose(out, (0, 2, 1, 3))[None]  4.15 us

profile of v1, /device:TPU:14, one launch (start us, length us, event | category | flops | bytes accessed | tf_op | source)
XLA Modules:
  0.0 131.3 jit_solution(7632712269121977289)
XLA Ops:
  0.0 1.4 %copy.11.routes_ref = s32[2,64,1]{2,1,0:T(8,128)} copy(s32[2,64,1]{1,0,2:T(2,128)} %bitcast.23) | data formatting | bytes 1024 | tf_op jit(solution)/shard_map/squeeze | solution.py:385
  1.4 1.4 %copy.12.gates_ref = f32[2,64,1]{2,1,0:T(8,128)} copy(f32[2,64,1]{1,0,2:T(2,128)} %bitcast.24) | data formatting | bytes 1024 | tf_op jit(solution)/shard_map/squeeze | solution.py:386
  2.8 1.8 %copy.18 = bf16[1,24,4,1792]{3,1,2,0:T(8,128)(2,1)} copy(bf16[1,24,4,1792]{3,2,1,0:T(4,128)(2,1)} %param.9) | data formatting | bytes 688128 | tf_op args[1]
  4.6 0.0 copy-start
  4.6 3.1 %copy.17 = bf16[2,64,4,1792]{3,1,2,0:T(8,128)(2,1)} copy(bf16[2,64,4,1792]{3,2,1,0:T(4,128)(2,1)} %param.8) | data formatting | bytes 3670016 | tf_op args[0]
  7.6 0.0 copy-done
  7.7 2.8 %copy.14 = bf16[224,8,2,512]{3,1,2,0:T(8,128)(2,1)} copy(bf16[224,8,2,512]{3,2,1,0:T(2,128)(2,1)S(1)} %bitcast.20) | data formatting | bytes 7340032
  10.4 116.7 %shard_map.82 = bf16[2,4,64,1792]{3,2,1,0:T(8,128)(2,1)} custom-call(bf16[2,4,64,1792]{3,2,1,0:T(8,128)(2,1)} %bitcast.19, bf16[4,24,1792]{2,1,0:T(8,128)(2,1)} %bitcast.22, f32[1,24]{1,0:T(1,128)} %bias_ref.1, bf16[1,1792]{1,0:T(2,128)(2,1)} %gain_ref.1, bf16[1792,1024]{1,0:T(8,128)(2,1)} %bitcast.17, bf16[512,1792]{1,0:T(8,128)(2,1)} %bitcast.21, ...), custom_call_target="tpu_custom_call" | custom-call | tf_op jit(solution)/shard_map/pallas_call | solution.py:371
  127.2 4.1 %copy.13 = bf16[1,2,64,4,1792]{4,3,2,1,0:T(4,128)(2,1)} copy(bf16[1,2,64,4,1792]{4,2,3,1,0:T(8,128)(2,1)} %bitcast.18) | data formatting | bytes 3670016 | tf_op jit(solution)/shard_map/broadcast_in_dim | solution.py:388
Async XLA Ops:
  4.6 3.1 %copy-start = (bf16[1,1,1792,2,512]{4,3,2,1,0:T(2,128)(2,1)S(1)}, bf16[1,1,1792,2,512]{4,3,2,1,0:T(2,128)(2,1)}, u32[]{:S(2)}) copy-start(bf16[1,1,1792,2,512]{4,3,2,1,0:T(2,128)(2,1)} %param.12) | copy-start | bytes 11010052

commit v2 on v1

--- a/solution.py
+++ b/solution.py
@@ -91,7 +91,7 @@
                 remote(branch.at[m], in_branch.at[m, layer], se_s.at[m, 0, 1],
                        se_r.at[m, layer, 1], "section", layer).wait_recv()
 
-                @pl.loop(0, width // LANES)
+                @pl.loop(0, width // LANES, unroll=True)
                 def _(c):
                     cols, res = mixed(m, c, lambda s: in_branch[m, layer, :, s].astype(F32))
                     for j in range(streams):
@@ -104,9 +104,11 @@
             projected = projected + lax.dot_general(
                 proj_ref[j], pj, NT, preferred_element_type=F32
             )
+            above = path[m, : j + 1].reshape((j + 1) * rows, width)
+            g = lax.dot_general(above, pj, NT, preferred_element_type=F32)
             for i in range(j + 1):
-                g = lax.dot_general(path[m, i], pj, NT, preferred_element_type=F32)
-                stats[m, dp, at : at + 1, :] = jnp.sum(jnp.where(eye, g, 0.0), axis=0, keepdims=True)
+                block = jnp.where(eye, g[i * rows : (i + 1) * rows], 0.0)
+                stats[m, dp, at : at + 1, :] = jnp.sum(block, axis=0, keepdims=True)
                 at += 1
         stats[m, dp, :coefs, :] = projected
         if m == 0:
@@ -165,7 +167,7 @@
             lax.broadcasted_iota(jnp.int32, (slots, rows), 0).astype(F32) == slotrow
         ).astype(F32).astype(BF16)
 
-        @pl.loop(0, width // LANES)
+        @pl.loop(0, width // LANES, unroll=True)
         def _(c):
             cols = pl.ds(pl.multiple_of(c * LANES, LANES), LANES)
             merged = tab[pre0] * path[m, 0, :, cols].astype(F32)
@@ -220,7 +222,7 @@
             load_gu.wait()
         tile = 256
 
-        @pl.loop(0, 2 * inner // tile)
+        @pl.loop(0, 2 * inner // tile, unroll=True)
         def _(c):
             cols = pl.ds(pl.multiple_of(c * tile, tile), tile)
             product = jnp.dot(
@@ -256,7 +258,7 @@
             load_d.wait()
         tile = 256 if width % 256 == 0 else LANES
 
-        @pl.loop(0, width // tile)
+        @pl.loop(0, width // tile, unroll=True)
         def _(c):
             cols = pl.ds(pl.multiple_of(c * tile, tile), tile)
             product = jnp.dot(
@@ -283,7 +285,7 @@
         await_from(m, ret, (re_s, re_r), "expert", ex, n_ex)
         tile = 256 if width % 256 == 0 else LANES
 
-        @pl.loop(0, width // tile)
+        @pl.loop(0, width // tile, unroll=True)
         def _(c):
             cols = pl.ds(pl.multiple_of(c * tile, tile), tile)
             value = gates * jnp.dot(
@@ -294,7 +296,7 @@
 
         to_sections(m, branch, in_branch, 1, "start")
 
-        @pl.loop(0, width // LANES)
+        @pl.loop(0, width // LANES, unroll=True)
         def _(c):
             cols, res = mixed(m, c, lambda s: acc_branch[:, s])
             for j in range(streams):

time: 132 us -> 117 us (0.89)
  Pallas kernels: 117 us -> 102 us
    pallas_call x1, Pallas kernels: 117 us -> 102 us  [body(): pl.pallas_call(functools.partial(kernel, sizes), out_shape=jax.ShapeDtype...]
where the time goes in v2:
time: 117 us
  Pallas kernels  102 us (87%)
  local copies, waits for them, and re-layouts  14.6 us (12%)
    pallas_call x1, Pallas kernels, body(): pl.pallas_call(functools.partial(kernel, sizes), out_shape=jax.ShapeDtype...  102 us
    unnamed x5, local copies, waits for them, and re-layouts  7.63 us
    broadcast_in_dim x1, local copies, waits for them, and re-layouts, body(): return jnp.transpose(out, (0, 2, 1, 3))[None]  4.15 us

profile of v2, /device:TPU:14, one launch (start us, length us, event | category | flops | bytes accessed | tf_op | source)
XLA Modules:
  0.0 117.1 jit_solution(14118375787326171023)
XLA Ops:
  0.0 1.4 %copy.11.routes_ref = s32[2,64,1]{2,1,0:T(8,128)} copy(s32[2,64,1]{1,0,2:T(2,128)} %bitcast.23) | data formatting | bytes 1024 | tf_op jit(solution)/shard_map/squeeze | solution.py:387
  1.4 1.4 %copy.12.gates_ref = f32[2,64,1]{2,1,0:T(8,128)} copy(f32[2,64,1]{1,0,2:T(2,128)} %bitcast.24) | data formatting | bytes 1024 | tf_op jit(solution)/shard_map/squeeze | solution.py:388
  2.8 1.8 %copy.18 = bf16[1,24,4,1792]{3,1,2,0:T(8,128)(2,1)} copy(bf16[1,24,4,1792]{3,2,1,0:T(4,128)(2,1)} %param.9) | data formatting | bytes 688128 | tf_op args[1]
  4.6 0.0 copy-start
  4.6 3.1 %copy.17 = bf16[2,64,4,1792]{3,1,2,0:T(8,128)(2,1)} copy(bf16[2,64,4,1792]{3,2,1,0:T(4,128)(2,1)} %param.8) | data formatting | bytes 3670016 | tf_op args[0]
  7.6 0.0 copy-done
  7.7 2.8 %copy.14 = bf16[224,8,2,512]{3,1,2,0:T(8,128)(2,1)} copy(bf16[224,8,2,512]{3,2,1,0:T(2,128)(2,1)S(1)} %bitcast.20) | data formatting | bytes 7340032
  10.4 102.5 %shard_map.82 = bf16[2,4,64,1792]{3,2,1,0:T(8,128)(2,1)} custom-call(bf16[2,4,64,1792]{3,2,1,0:T(8,128)(2,1)} %bitcast.19, bf16[4,24,1792]{2,1,0:T(8,128)(2,1)} %bitcast.22, f32[1,24]{1,0:T(1,128)} %bias_ref.1, bf16[1,1792]{1,0:T(2,128)(2,1)} %gain_ref.1, bf16[1792,1024]{1,0:T(8,128)(2,1)} %bitcast.17, bf16[512,1792]{1,0:T(8,128)(2,1)} %bitcast.21, ...), custom_call_target="tpu_custom_call" | custom-call | tf_op jit(solution)/shard_map/pallas_call | solution.py:373
  112.9 4.1 %copy.13 = bf16[1,2,64,4,1792]{4,3,2,1,0:T(4,128)(2,1)} copy(bf16[1,2,64,4,1792]{4,2,3,1,0:T(8,128)(2,1)} %bitcast.18) | data formatting | bytes 3670016 | tf_op jit(solution)/shard_map/broadcast_in_dim | solution.py:390
Async XLA Ops:
  4.6 3.1 %copy-start = (bf16[1,1,1792,2,512]{4,3,2,1,0:T(2,128)(2,1)S(1)}, bf16[1,1,1792,2,512]{4,3,2,1,0:T(2,128)(2,1)}, u32[]{:S(2)}) copy-start(bf16[1,1,1792,2,512]{4,3,2,1,0:T(2,128)(2,1)} %param.12) | copy-start | bytes 11010052
